TPU v7x, 128 devices: a 2x2x16 block of a 8x8x16 slice. The times are simulated.
128 devices in a mesh: grp: 4 (over x, y), tok: 16 (over z), mdl: 2 (over core).
Axes of the slice: x: 2, y: 2, z: 16, core: 2. Of those that a mesh axis runs over, the one named last changes fastest.
The devices are a block of a 8x8x16 slice.
Arguments:
- hidden: bfloat16 [4096, 4096], P(('grp', 'tok'), 'mdl'), parts along dimension 0, may hold values from -3 to 3
- queries: bfloat16 [4096, 16, 128], P(('grp', 'tok'), 'mdl'), parts along dimension 0, may hold values from -8 to 8
- cache: bfloat16 [64, 2048, 4, 2, 128], P(('grp', 'tok'), None, 'mdl'), parts along dimension 0, may hold values from -8 to 8
- cache_lengths: int32 [64], P(('grp', 'tok')), parts along dimension 0, may hold values from 128 to 2048, as said below
- wkv: bfloat16 [4096, 4, 2, 128], P('tok', 'mdl'), may hold values from -0.09375 to 0.09375
- wo: bfloat16 [16, 128, 4096], P('mdl', None, 'tok'), may hold values from -0.5 to 0.5
- attn_gain: bfloat16 [4096], replicated, may hold values from 0.5 to 1.5
- moe_gain: bfloat16 [4096], replicated, may hold values from 0.5 to 1.5
- w_gate: bfloat16 [32, 4096, 896], P(('tok', 'mdl')), may hold values from -0.09375 to 0.09375
- w_up: bfloat16 [32, 4096, 896], P(('tok', 'mdl')), may hold values from -0.09375 to 0.09375
- w_down: bfloat16 [32, 896, 4096], P(('tok', 'mdl')), may hold values from -0.0625 to 0.0625
- expert_ids: int32 [4096, 2], P(('grp', 'tok', 'mdl')), parts along dimension 0, may hold values from 0 to 3, all different within a row; in each aligned block of 32 rows (0 to 31, 32 to 63, ...) at most 18 rows name the same one
- gates: float32 [4096, 2], P(('grp', 'tok', 'mdl')), parts along dimension 0, may hold values from 0.1 to 1
Outputs:
- mixed: bfloat16 [4096, 4096], P(('grp', 'tok', 'mdl')), parts along dimension 0
- fresh_key_value: bfloat16 [4096, 4, 2, 128], P(('grp', 'tok'), 'mdl'), parts along dimension 0
There are 4 independent parts, one for each index of `grp`. A program takes and returns all parts, laid end to end along the dimension named above; an argument that names none is the same for every part. Nothing has to cross between parts.
Inputs may be any that keep to these rules, and one draw needn't show every extreme that they name: `expert_ids`: each token names 2 different experts; in aligned blocks of 32 rows no expert is named by more than 18 rows, a bound that some block reaches. `cache_lengths`: some rollout holds exactly 2048 cached positions.
All inputs are finite; a program needn't handle non-finite values.
Results may differ from a plain program's by a relative error of at most 0.007.
Values may be sent and summed in bfloat16 or wider, within the bound.
A program may use at most 128 MiB of HBM per device.

v0:
```python
import math
import jax
import jax.numpy as jnp
from jax import lax
from jax.sharding import PartitionSpec as P

EXPERTS = 4
TOPK = 2
eps_norm = 1e-05
rope_base = 1000000.0
mask_fill = -1e30


def joined_along(tiles, dim):
    dims = list(tiles.shape[1:])
    dims[dim] *= tiles.shape[0]
    return jnp.moveaxis(tiles, 0, dim).reshape(dims)


def sent_to_all(shard, axis):
    copies = jnp.broadcast_to(shard, (lax.axis_size(axis), *shard.shape))
    return lax.all_to_all(copies, axis, split_axis=0, concat_axis=0, tiled=True)


def collect(shard, axis, dim):
    return joined_along(sent_to_all(shard, axis), dim)


def in_blocks(shard, dim, size):
    dims = shard.shape
    tiles = shard.reshape(*dims[:dim], size, dims[dim] // size, *dims[dim + 1 :])
    return jnp.moveaxis(tiles, dim, 0)


def sent_and_summed(shard, axis, dim):
    tiles = in_blocks(shard, dim, lax.axis_size(axis))
    arrived = lax.all_to_all(tiles, axis, split_axis=0, concat_axis=0, tiled=True)
    return arrived.sum(axis=0)


def sent_and_summed_2(shard, axis, dim):
    size = lax.axis_size(axis)
    tiles = lax.all_to_all(in_blocks(shard, dim, size), axis, 0, 0, tiled=True)
    return jnp.sum(tiles.astype(jnp.float32), axis=0)


def rms_scale(values_in, gain):
    values = values_in.astype(jnp.float32)
    meansq = jnp.mean(values * values, axis=-1, keepdims=True)
    return values * lax.rsqrt(meansq + eps_norm) * gain.astype(jnp.float32)


def rotate(key_rows, positions):
    half_dim = key_rows.shape[-1] // 2
    inverse = jnp.exp(
        jnp.arange(half_dim, dtype=jnp.float32) * (-2.0 * math.log(rope_base) / key_rows.shape[-1])
    )
    angle = positions.astype(jnp.float32)[:, None] * inverse[None, :]
    cosine = jnp.cos(angle)[:, None, :]
    sine_vals = jnp.sin(angle)[:, None, :]
    front_half = key_rows[..., :half_dim]
    back_half = key_rows[..., half_dim:]
    return jnp.concatenate(
        [front_half * cosine - back_half * sine_vals, back_half * cosine + front_half * sine_vals],
        axis=-1,
    )


def score_rows(query_rows, key_rows, scale_factor):
    return (
        lax.dot_general(
            query_rows, key_rows, (((1,), (1,)), ((), ())), preferred_element_type=jnp.float32
        )
        * scale_factor
    )


def head_attention(query_rows, cache_keys, cache_values, length, new_keys, new_values, head_group):
    row_count = query_rows.shape[0]
    block_len = min(512, cache_keys.shape[0])
    scale_factor = 1.0 / math.sqrt(query_rows.shape[1])
    token_of_row = jnp.arange(row_count) // head_group
    block_total = (length + block_len - 1) // block_len

    def block_scores(block_idx):
        row_offset = block_idx * block_len
        block_keys = lax.dynamic_slice_in_dim(cache_keys, row_offset, block_len, 0)
        allowed = row_offset + jnp.arange(block_len) < length
        return (
            jnp.where(
                allowed[None, :], score_rows(query_rows, block_keys, scale_factor), mask_fill
            ),
            allowed,
        )

    new_allowed = jnp.arange(new_keys.shape[0])[None, :] <= token_of_row[:, None]
    new_scores = jnp.where(new_allowed, score_rows(query_rows, new_keys, scale_factor), mask_fill)
    first_max = jnp.max(new_scores, axis=1)
    first_sum = jnp.sum(
        jnp.where(new_allowed, jnp.exp(new_scores - first_max[:, None]), 0.0), axis=1
    )

    def first_pass(block_idx, carry):
        run_max, run_sum = carry
        scores, allowed = block_scores(block_idx)
        next_max = jnp.maximum(run_max, jnp.max(scores, axis=1))
        weights = jnp.where(allowed[None, :], jnp.exp(scores - next_max[:, None]), 0.0)
        return (next_max, run_sum * jnp.exp(run_max - next_max) + jnp.sum(weights, axis=1))

    row_max, row_sum = lax.fori_loop(0, block_total, first_pass, (first_max, first_sum))
    new_probs = (
        jnp.where(new_allowed, jnp.exp(new_scores - row_max[:, None]), 0.0) / row_sum[:, None]
    ).astype(jnp.bfloat16)
    start_total = jnp.dot(new_probs, new_values, preferred_element_type=jnp.float32)

    def second_pass(block_idx, total):
        scores, allowed = block_scores(block_idx)
        probs = (
            jnp.where(allowed[None, :], jnp.exp(scores - row_max[:, None]), 0.0) / row_sum[:, None]
        ).astype(jnp.bfloat16)
        block_values = lax.dynamic_slice_in_dim(cache_values, block_idx * block_len, block_len, 0)
        return total + jnp.dot(probs, block_values, preferred_element_type=jnp.float32)

    total = lax.fori_loop(0, block_total, second_pass, start_total)
    return total.astype(jnp.bfloat16)


def shards(
    hidden,
    queries,
    cache,
    cache_lengths,
    wkv,
    wo,
    attn_gain,
    moe_gain,
    w_gate,
    w_up,
    w_down,
    expert_ids,
    gates,
):
    full_rows = collect(hidden, "mdl", 1)
    span_len = full_rows.shape[0]
    normalized_input = rms_scale(full_rows, attn_gain).astype(jnp.bfloat16)
    kv_heads = wkv.shape[1]
    head_dim = wkv.shape[3]
    weight_piece = lax.all_gather(wkv, "tok", axis=0, tiled=True)
    key_value_projection = jnp.dot(
        normalized_input,
        weight_piece.reshape(weight_piece.shape[0], -1),
        preferred_element_type=jnp.float32,
    ).reshape(span_len, kv_heads, 2, head_dim)
    length = cache_lengths[0]
    positions = length + jnp.arange(span_len, dtype=jnp.int32)
    fresh_key_value = jnp.stack(
        [rotate(key_value_projection[:, :, 0], positions), key_value_projection[:, :, 1]], axis=2
    ).astype(jnp.bfloat16)
    head_group = queries.shape[1] // kv_heads
    outputs = []
    for head_index in range(kv_heads):
        query_rows = queries[:, head_index * head_group : (head_index + 1) * head_group].reshape(
            span_len * head_group, head_dim
        )
        attended = head_attention(
            query_rows,
            cache[0, :, head_index, 0],
            cache[0, :, head_index, 1],
            length,
            fresh_key_value[:, head_index, 0],
            fresh_key_value[:, head_index, 1],
            head_group,
        )
        outputs.append(attended.reshape(span_len, head_group * head_dim))
    heads_out = jnp.concatenate(outputs, axis=1)
    weight_piece = lax.all_gather(wo, "tok", axis=2, tiled=True)
    attn_out = jnp.dot(
        heads_out,
        weight_piece.reshape(-1, weight_piece.shape[2]),
        preferred_element_type=jnp.float32,
    )
    core_rows = span_len // lax.axis_size("mdl")
    core_start = lax.axis_index("mdl") * core_rows
    attn_rows = sent_and_summed(attn_out, "mdl", 0)
    resid = (
        lax.dynamic_slice_in_dim(full_rows, core_start, core_rows, 0).astype(jnp.float32)
        + attn_rows
    )
    moe_in = rms_scale(resid, moe_gain).astype(jnp.bfloat16)
    expert_range = jnp.arange(EXPERTS)
    matches = expert_ids[:, :, None] == expert_range[None, None, :]
    chosen = jnp.sum(matches.astype(jnp.int32), axis=1)
    route = jnp.sum(jnp.where(matches, gates[:, :, None], 0.0), axis=1)
    slot_of = jnp.cumsum(chosen, axis=0) - chosen
    capacity = core_rows * TOPK * 9 // (8 * EXPERTS)
    slot_range = jnp.arange(capacity)
    select = (slot_of.T[:, None, :] == slot_range[None, :, None]) & (chosen.T[:, None, :] > 0)
    send_rows = jnp.einsum(
        "eci,id->ecd", select.astype(jnp.bfloat16), moe_in, preferred_element_type=jnp.float32
    ).astype(jnp.bfloat16)
    owners = lax.axis_size("tok") * lax.axis_size("mdl")
    slabs = owners // EXPERTS
    model_width = moe_in.shape[1]
    core_count = lax.axis_size("mdl")
    send_chip = jnp.repeat(send_rows, slabs // core_count, axis=0)
    received = lax.all_to_all(send_chip, "tok", split_axis=0, concat_axis=0, tiled=True)
    chip_count = received.shape[0]
    item_count = received.shape[1]
    both_cores = collect(received[:, None], "mdl", 1)
    received = both_cores.reshape(-1, item_count, model_width)
    flat_rows = received.reshape(-1, model_width)
    gate_val = jnp.dot(flat_rows, w_gate[0], preferred_element_type=jnp.float32)
    up_val = jnp.dot(flat_rows, w_up[0], preferred_element_type=jnp.float32)
    slab_hidden = (jax.nn.silu(gate_val) * up_val).astype(jnp.bfloat16)
    slab_out = jnp.dot(slab_hidden, w_down[0], preferred_element_type=jnp.float32).astype(
        jnp.bfloat16
    )
    slab_out = slab_out.reshape(received.shape)
    per_core = slab_out.reshape(chip_count, core_count, item_count, model_width).astype(jnp.float32)
    chip_total = sent_and_summed_2(per_core.astype(jnp.bfloat16), "mdl", 1)
    returned = lax.all_to_all(
        chip_total[:, 0].astype(jnp.bfloat16), "tok", split_axis=0, concat_axis=0, tiled=True
    ).astype(jnp.float32)
    summed = jnp.sum(returned.reshape(EXPERTS, slabs // core_count, capacity, model_width), axis=1)
    weight_table = select.astype(jnp.float32) * route.T[:, None, :]
    moe_out = jnp.einsum("eci,ecd->id", weight_table, summed, precision=lax.Precision.HIGHEST)
    mixed = (resid + moe_out).astype(jnp.bfloat16)
    return (mixed, fresh_key_value)


def solution(mesh):
    in_specs = (
        P(("grp", "tok"), "mdl"),
        P(("grp", "tok"), "mdl", None),
        P(("grp", "tok"), None, "mdl", None, None),
        P(("grp", "tok")),
        P("tok", "mdl", None, None),
        P("mdl", None, "tok"),
        P(),
        P(),
        P(("tok", "mdl"), None, None),
        P(("tok", "mdl"), None, None),
        P(("tok", "mdl"), None, None),
        P(("grp", "tok", "mdl"), None),
        P(("grp", "tok", "mdl"), None),
    )
    out_specs = (P(("grp", "tok", "mdl"), None), P(("grp", "tok"), "mdl", None, None))
    return jax.shard_map(shards, mesh=mesh, in_specs=in_specs, out_specs=out_specs, check_vma=False)
```

profile of v0, /device:TPU:84, one launch (start us, length us, event | category | flops | bytes accessed | tf_op | source)
XLA Modules:
  0.0 608.0 jit_solution(13349930791535107725)
XLA Ops:
  8.1 0.7 all-gather.5.cloned.1.call-update
  8.8 1.8 broadcast_in_dim.140
  10.6 3.5 all-to-all-start
  16.9 1.2 reshape.194
  18.7 3.0 fusion.112
  21.7 0.9 copy_bitcast_fusion.2
  22.8 67.3 %all-gather.3.cloned.1.call-done = bf16[4096,2,2,128]{3,2,1,0:T(2,128)(2,1)} async-done(((bf16[256,2,2,128]{3,2,1,0:T(2,128)(2,1)}), bf16[4096,2,2,128]{3,2,1,0:T(2,128)(2,1)}) %all-gather.3.cloned.1.call-update) | async-done | bytes 4194320 | tf_op jit(solution)/shard_map/all_gather | solution.py:148
  90.1 11.2 %copy.122 = bf16[4096,2,2,128]{0,3,2,1:T(8,128)(2,1)} copy(bf16[4096,2,2,128]{3,2,1,0:T(2,128)(2,1)} %all-gather.3.cloned.1.call-done) | data formatting | bytes 8388608 | tf_op jit(solution)/shard_map/reshape | solution.py:151
  101.2 3.7 fusion.116
  105.5 1.1 while.44
  106.9 2.1 while.45
  107.6 1.4 fusion.144
  109.1 1.1 while.46
  110.5 1.2 while.47
  111.8 101.1 %all-gather.5.cloned.1.call-done = bf16[8,128,4096]{2,1,0:T(8,128)(2,1)} async-done(((bf16[8,128,256]{2,1,0:T(8,128)(2,1)}), bf16[8,128,4096]{2,1,0:T(8,128)(2,1)}) %all-gather.5.cloned.1.call-update) | async-done | bytes 8388624 | tf_op jit(solution)/shard_map/all_gather | solution.py:176
  212.9 5.0 fusion.80
  217.9 4.6 all_to_all.30
  223.7 149.6 %all_to_all.31 = bf16[16,18,4096]{2,1,0:T(8,128)(2,1)S(1)} all-to-all(bf16[16,18,4096]{2,1,0:T(8,128)(2,1)S(1)} %bitcast.122), channel_id=1, replica_groups=mesh['grp'=4,'tok'=16,'mdl'=2] {'tok'}, dimensions={0} | all-to-all | bytes 4718592 | tf_op jit(solution)/shard_map/all_to_all | solution.py:206
  373.3 1.3 copy.114
  375.2 7.7 %all_to_all.32 = bf16[2,16,1,18,4096]{4,1,3,2,0:T(8,128)(2,1)S(1)} all-to-all(bf16[2,16,1,18,4096]{4,1,3,2,0:T(8,128)(2,1)S(1)} %broadcast_in_dim.146), channel_id=1, replica_groups=mesh['grp'=4,'tok'=16,'mdl'=2] {'mdl'}, dimensions={0} | all-to-all | bytes 9437184 | tf_op jit(solution)/shard_map/all_to_all | solution.py:22
  382.9 5.4 copy.115
  388.3 7.8 %reshape_reshape_reshape.3 = bf16[576,4096]{1,0:T(8,128)(2,1)} reshape(bf16[16,2,1,18,4096]{4,3,1,0,2:T(8,128)(2,1)} %copy.115) | data formatting | bytes 9437184 | tf_op jit(solution)/shard_map/reshape;reshape;reshape | solution.py:211
  396.1 10.7 %fusion.54 = f32[576,896]{1,0:T(8,128)S(1)} fusion(bf16[576,4096]{1,0:T(8,128)(2,1)} %reshape_reshape_reshape.3, bf16[1,4096,896]{2,1,0:T(8,128)(2,1)} %param.29), kind=kOutput, calls=%fused_computation.62 | convolution fusion | flops 4227858432 | bytes 14123008 | tf_op jit(solution)/shard_map/dot_general | solution.py:212
  406.8 17.4 %fusion.56 = bf16[576,4096]{1,0:T(8,128)(2,1)} fusion(bf16[1,896,4096]{2,1,0:T(8,128)(2,1)} %param.31, f32[576,896]{1,0:T(8,128)S(1)} %fusion.54, bf16[576,4096]{1,0:T(8,128)(2,1)} %reshape_reshape_reshape.3, bf16[1,4096,896]{2,1,0:T(8,128)(2,1)} %param.30), kind=kOutput, calls=%fused_computation.65 | convolution fusion | flops 8461172736 | bytes 26181632 | tf_op jit(solution)/shard_map/dot_general | solution.py:215
  424.2 7.6 %reshape.188 = bf16[16,2,1,18,4096]{4,3,1,0,2:T(8,128)(2,1)} reshape(bf16[576,4096]{1,0:T(8,128)(2,1)} %fusion.56) | data formatting | bytes 9437184 | tf_op jit(solution)/shard_map/reshape | solution.py:31
  431.8 5.4 copy.116
  437.2 8.6 %all_to_all.33 = bf16[2,16,1,18,4096]{4,1,3,2,0:T(8,128)(2,1)} all-to-all(bf16[2,16,1,18,4096]{4,1,3,2,0:T(8,128)(2,1)S(1)} %copy.116), channel_id=1, replica_groups=mesh['grp'=4,'tok'=16,'mdl'=2] {'mdl'}, dimensions={0} | all-to-all | bytes 9437184 | tf_op jit(solution)/shard_map/all_to_all | solution.py:43
  445.8 3.6 reduce_sum.109
  449.4 3.1 copy.117
  452.5 6.5 %all-to-all-start.5 = ((bf16[16,18,4096]{2,1,0:T(8,128)(2,1)}), bf16[16,18,4096]{2,1,0:T(8,128)(2,1)S(1)}, u32[]{:S(2)}, u32[]{:S(2)}) async-start(bf16[16,18,4096]{2,1,0:T(8,128)(2,1)} %copy.117), calls=%async_computation.5 | async-start | bytes 6291456 | tf_op jit(solution)/shard_map/all_to_all | solution.py:221
  459.8 138.6 %all-to-all-done.5 = bf16[16,18,4096]{2,1,0:T(8,128)(2,1)S(1)} async-done(((bf16[16,18,4096]{2,1,0:T(8,128)(2,1)}), bf16[16,18,4096]{2,1,0:T(8,128)(2,1)S(1)}, u32[]{:S(2)}, u32[]{:S(2)}) %all-to-all-start.5) | async-done | bytes 2359328 | tf_op jit(solution)/shard_map/all_to_all | solution.py:221
  599.6 1.6 fusion.60
  (81 shorter events, 12.4 us)
Async XLA Ops:
  7.2 10.9 %copy-start.8 = (s32[32,2]{0,1:T(2,128)S(1)}, s32[32,2]{0,1:T(2,128)}, u32[]{:S(2)}) copy-start(s32[32,2]{0,1:T(2,128)} %param.32) | copy-start | bytes 772
  7.2 11.2 %copy-start.7 = (bf16[4096]{0:T(1024)(128)(2,1)S(1)}, bf16[4096]{0:T(1024)(128)(2,1)}, u32[]{:S(2)}) copy-start(bf16[4096]{0:T(1024)(128)(2,1)} %param.28) | copy-start | bytes 24580
  7.2 11.4 %copy-start.6 = (bf16[64,8,128]{2,1,0:T(8,128)(2,1)S(1)}, bf16[64,8,128]{2,1,0:T(8,128)(2,1)}, u32[]{:S(2)}) copy-start(bf16[64,8,128]{2,1,0:T(8,128)(2,1)} %param.22) | copy-start | bytes 393220
  7.2 11.5 %copy-start.2 = (bf16[1,2048,2,2,128]{4,3,2,1,0:T(2,128)(2,1)S(1)}, bf16[1,2048,2,2,128]{4,3,2,1,0:T(2,128)(2,1)}, u32[]{:S(2)}) copy-start(bf16[1,2048,2,2,128]{4,3,2,1,0:T(2,128)(2,1)} %param.23) | copy-start | bytes 6291460
  7.2 82.8 %all-gather.3.cloned.1.call-start = ((), (), s32[]{:S(2)}) async-start(), calls=%async_computation.6 | async-start | bytes 4456448 | tf_op jit(solution)/shard_map/all_gather | solution.py:148
  8.0 204.9 %all-gather.5.cloned.1.call-start = ((), (), s32[]{:S(2)}) async-start(), calls=%async_computation.7 | async-start | bytes 8912896 | tf_op jit(solution)/shard_map/all_gather | solution.py:176
  10.6 5.2 all-to-all-start
  18.1 204.7 %copy-start.3 = (bf16[2,8,8,2048]{3,2,0,1:T(8,128)(2,1)}, bf16[2,8,8,2048]{3,2,0,1:T(8,128)(2,1)S(1)}, u32[]{:S(2)}) copy-start(bf16[2,8,8,2048]{3,2,0,1:T(8,128)(2,1)S(1)} %copy.129) | copy-start | bytes 1572868
  22.8 78.5 %copy-start.5 = (bf16[64,4096,1,1]{1,0,2,3:T(8,128)(2,1)S(1)}, bf16[64,4096,1,1]{1,0,2,3:T(8,128)(2,1)}, u32[]{:S(2)}) copy-start(bf16[64,4096,1,1]{1,0,2,3:T(8,128)(2,1)} %reshape.194) | copy-start | bytes 1572868
  222.6 150.7 %copy-start = (f32[32,4096]{1,0:T(8,128)}, f32[32,4096]{1,0:T(8,128)S(1)}, u32[]{:S(2)}) copy-start(f32[32,4096]{1,0:T(8,128)S(1)} %reduce_sum.105) | copy-start | bytes 1572868
  449.4 9.6 %copy-start.9 = (f32[32,2]{0,1:T(2,128)S(1)}, f32[32,2]{0,1:T(2,128)}, u32[]{:S(2)}) copy-start(f32[32,2]{0,1:T(2,128)} %param.33) | copy-start | bytes 772
  452.5 145.9 %all-to-all-start.5 = ((bf16[16,18,4096]{2,1,0:T(8,128)(2,1)}), bf16[16,18,4096]{2,1,0:T(8,128)(2,1)S(1)}, u32[]{:S(2)}, u32[]{:S(2)}) async-start(bf16[16,18,4096]{2,1,0:T(8,128)(2,1)} %copy.117), calls=%async_computation.5 | async-start | bytes 6291456 | tf_op jit(solution)/shard_map/all_to_all | solution.py:221
  598.4 1.0 copy-start.1
  598.4 1.2 copy-start.4
Sparse Core Ops, SparseCore 0:
  9.7 80.3 all-gather.2
  91.7 121.2 all-gather.4
where the time goes:
time: 609 us; the launch traced here: 608 us
  waiting for transfers between devices  309 us (51%)
  blocking collectives  171 us (28%)
  local copies, waits for them, and re-layouts  52.8 us (9%)
  matrix products  42.1 us (7%)
  between operations  15.1 us (2%)
  starting transfers between devices  10.2 us (2%)
  other arithmetic  8.38 us (1%)
    all_to_all x1, blocking collectives, shards(): lax.all_to_all(send_chip, 'tok', split_axis=0, concat_axis=0, tiled=True)  150 us
    all_to_all x1, waiting for transfers between devices, shards(): lax.all_to_all(chip_total[:, 0].astype(jnp.bfloat16), 'tok', split_axis=0...  139 us
    all_gather x1, waiting for transfers between devices, shards(): weight_piece = lax.all_gather(wo, 'tok', axis=2, tiled=True)  101 us
    all_gather x1, waiting for transfers between devices, shards(): weight_piece = lax.all_gather(wkv, 'tok', axis=0, tiled=True)  67.3 us
    dot_general x1, matrix products, shards(): jnp.dot(slab_hidden, w_down[0], preferred_element_type=jnp.float32)  17.4 us
  transfers between devices with their start and end apart: 4, of which 4 were waited for; matrix products, arithmetic and copies ran while one was open for 5% of the time, Pallas kernels for 0%

commit v1 on v0

--- a/solution.py
+++ b/solution.py
@@ -1,14 +1,23 @@
+import functools
 import math
 import jax
 import jax.numpy as jnp
 from jax import lax
 from jax.sharding import PartitionSpec as P
+from jax.lax import all_to_all, axis_size
 
 EXPERTS = 4
 TOPK = 2
 eps_norm = 1e-05
 rope_base = 1000000.0
 mask_fill = -1e30
+
+
+def _serve_screen(arr, dim_no):
+    return jnp.concatenate(all_to_all(jnp.stack([arr] * axis_size("tok"), 0), "tok", 0, 0), dim_no)
+
+
+play_modes_now = functools.partial(_serve_screen, dim_no=2)
 
 
 def joined_along(tiles, dim):
@@ -173,7 +182,7 @@
         )
         outputs.append(attended.reshape(span_len, head_group * head_dim))
     heads_out = jnp.concatenate(outputs, axis=1)
-    weight_piece = lax.all_gather(wo, "tok", axis=2, tiled=True)
+    weight_piece = play_modes_now(wo)
     attn_out = jnp.dot(
         heads_out,
         weight_piece.reshape(-1, weight_piece.shape[2]),

time: 609 us -> 870 us (1.43)
  waiting for transfers between devices: 309 us -> 513 us
  local copies, waits for them, and re-layouts: 52.8 us -> 82.1 us
  starting transfers between devices: 10.2 us -> 23.7 us
    all_gather x1, waiting for transfers between devices: 67.3 us -> 345 us  [shards(): weight_piece = lax.all_gather(wkv, 'tok', axis=0, tiled=True)]
    all_gather x1 -> x0, waiting for transfers between devices: 101 us -> none  [shards(): weight_piece = lax.all_gather(wo, 'tok', axis=2, tiled=True)]
    all_to_all x1, waiting for transfers between devices: 0.34 us -> 28.5 us  [_serve_screen(): all_to_all(jnp.stack([arr] * axis_size('tok'), 0), 'tok', 0, 0)]
    another operation x0 -> x2, local copies, waits for them, and re-layouts: none -> 18.8 us  [the longest x1 13.5 us: shards(): weight_piece.reshape(-1, weight_piece.shape[2])]
    all_to_all x1, starting transfers between devices: 3.52 us -> 17.2 us  [_serve_screen(): all_to_all(jnp.stack([arr] * axis_size('tok'), 0), 'tok', 0, 0)]
    reshape x0 -> x1, local copies, waits for them, and re-layouts: none -> 11.8 us  [_serve_screen(): jnp.concatenate(all_to_all(jnp.stack([arr] * axis_size('tok'), 0), 'tok',...]
  transfers between devices with their start and end apart: 4 -> 3, of which waited for: 4 -> 3; matrix products, arithmetic and copies ran while one was open for 5% -> 3% of each run, Pallas kernels for 0% -> 0%
where the time goes in v1:
time: 870 us; the launch traced here: 862 us
  waiting for transfers between devices  513 us (59%)
  blocking collectives  177 us (20%)
  local copies, waits for them, and re-layouts  82.1 us (9%)
  matrix products  42 us (5%)
  starting transfers between devices  23.7 us (3%)
  between operations  15.3 us (2%)
    all_gather x1, waiting for transfers between devices, shards(): weight_piece = lax.all_gather(wkv, 'tok', axis=0, tiled=True)  345 us
    all_to_all x1, blocking collectives, shards(): lax.all_to_all(send_chip, 'tok', split_axis=0, concat_axis=0, tiled=True)  152 us
    all_to_all x1, waiting for transfers between devices, shards(): lax.all_to_all(chip_total[:, 0].astype(jnp.bfloat16), 'tok', split_axis=0...  139 us
    all_to_all x1, waiting for transfers between devices, _serve_screen(): all_to_all(jnp.stack([arr] * axis_size('tok'), 0), 'tok', 0, 0)  28.5 us
    dot_general x1, matrix products, shards(): jnp.dot(slab_hidden, w_down[0], preferred_element_type=jnp.float32)  17.4 us
  transfers between devices with their start and end apart: 3, of which 3 were waited for; matrix products, arithmetic and copies ran while one was open for 3% of the time, Pallas kernels for 0%

profile of v1, /device:TPU:84, one launch (start us, length us, event | category | flops | bytes accessed | tf_op | source)
XLA Modules:
  0.0 862.4 jit_solution(16127130322035127063)
XLA Ops:
  8.2 4.2 all_to_all.35
  12.3 5.3 stack.9
  17.7 17.2 %all-to-all-start.1 = ((bf16[16,8,128,256]{3,2,1,0:T(8,128)(2,1)}), bf16[16,8,128,256]{3,2,1,0:T(8,128)(2,1)}, u32[]{:S(2)}, u32[]{:S(2)}) async-start(bf16[16,8,128,256]{3,2,1,0:T(8,128)(2,1)} %stack.9), calls=%async_computation.1 | async-start | bytes 16777216 | tf_op jit(solution)/shard_map/all_to_all | solution.py:17
  37.4 1.2 reshape.196
  39.2 3.0 fusion.112
  43.3 345.2 %all-gather.2.cloned.1.call-done = bf16[4096,2,2,128]{3,2,1,0:T(2,128)(2,1)} async-done(((bf16[256,2,2,128]{3,2,1,0:T(2,128)(2,1)}), bf16[4096,2,2,128]{3,2,1,0:T(2,128)(2,1)}) %all-gather.2.cloned.1.call-update) | async-done | bytes 4194320 | tf_op jit(solution)/shard_map/all_gather | solution.py:157
  388.5 11.2 %copy.127 = bf16[4096,2,2,128]{0,3,2,1:T(8,128)(2,1)} copy(bf16[4096,2,2,128]{3,2,1,0:T(2,128)(2,1)} %all-gather.2.cloned.1.call-done) | data formatting | bytes 8388608 | tf_op jit(solution)/shard_map/reshape | solution.py:160
  399.8 3.6 fusion.116
  405.3 2.1 while.47
  406.0 1.4 fusion.150
  407.5 1.1 while.44
  408.9 1.7 while.45
  410.7 28.5 %all-to-all-done.1 = bf16[16,8,128,256]{3,2,1,0:T(8,128)(2,1)} async-done(((bf16[16,8,128,256]{3,2,1,0:T(8,128)(2,1)}), bf16[16,8,128,256]{3,2,1,0:T(8,128)(2,1)}, u32[]{:S(2)}, u32[]{:S(2)}) %all-to-all-start.1) | async-done | bytes 8388640 | tf_op jit(solution)/shard_map/all_to_all | solution.py:17
  439.2 11.8 %copy.115 = bf16[8,128,16,256]{3,2,1,0:T(8,128)(2,1)} copy(bf16[8,128,16,256]{3,1,0,2:T(8,128)(2,1)} %bitcast.20) | data formatting | bytes 16777216 | tf_op jit(solution)/shard_map/reshape | solution.py:17
  451.0 13.5 %reshape.197 = bf16[1024,4096,1]{1,0,2:T(8,128)(2,1)} reshape(bf16[8,128,16,256]{3,2,1,0:T(8,128)(2,1)} %copy.115) | data formatting | bytes 16777216 | tf_op jit(solution)/shard_map/reshape;reshape | solution.py:188
  464.4 5.0 fusion.80
  469.4 4.6 all_to_all.36
  475.2 152.1 %all_to_all.37 = bf16[16,18,4096]{2,1,0:T(8,128)(2,1)S(1)} all-to-all(bf16[16,18,4096]{2,1,0:T(8,128)(2,1)S(1)} %bitcast.122), channel_id=1, replica_groups=mesh['grp'=4,'tok'=16,'mdl'=2] {'tok'}, dimensions={0} | all-to-all | bytes 4718592 | tf_op jit(solution)/shard_map/all_to_all | solution.py:215
  627.3 1.3 copy.119
  629.2 7.7 all_to_all.38
  636.9 5.4 copy.120
  642.3 7.8 reshape_reshape_reshape.3
  650.1 10.7 %fusion.54 = f32[576,896]{1,0:T(8,128)S(1)} fusion(bf16[576,4096]{1,0:T(8,128)(2,1)} %reshape_reshape_reshape.3, bf16[1,4096,896]{2,1,0:T(8,128)(2,1)} %param.29), kind=kOutput, calls=%fused_computation.62 | convolution fusion | flops 4227858432 | bytes 14123008 | tf_op jit(solution)/shard_map/dot_general | solution.py:221
  660.8 17.4 %fusion.56 = bf16[576,4096]{1,0:T(8,128)(2,1)} fusion(bf16[1,896,4096]{2,1,0:T(8,128)(2,1)} %param.31, f32[576,896]{1,0:T(8,128)S(1)} %fusion.54, bf16[576,4096]{1,0:T(8,128)(2,1)} %reshape_reshape_reshape.3, bf16[1,4096,896]{2,1,0:T(8,128)(2,1)} %param.30), kind=kOutput, calls=%fused_computation.65 | convolution fusion | flops 8461172736 | bytes 26181632 | tf_op jit(solution)/shard_map/dot_general | solution.py:224
  678.2 7.8 reshape.190
  686.0 5.4 copy.121
  691.4 8.6 %all_to_all.39 = bf16[2,16,1,18,4096]{4,1,3,2,0:T(8,128)(2,1)} all-to-all(bf16[2,16,1,18,4096]{4,1,3,2,0:T(8,128)(2,1)S(1)} %copy.121), channel_id=1, replica_groups=mesh['grp'=4,'tok'=16,'mdl'=2] {'mdl'}, dimensions={0} | all-to-all | bytes 9437184 | tf_op jit(solution)/shard_map/all_to_all | solution.py:52
  700.0 3.6 reduce_sum.109
  703.6 3.1 copy.122
  706.7 6.5 all-to-all-start.6
  713.9 138.6 %all-to-all-done.6 = bf16[16,18,4096]{2,1,0:T(8,128)(2,1)S(1)} async-done(((bf16[16,18,4096]{2,1,0:T(8,128)(2,1)}), bf16[16,18,4096]{2,1,0:T(8,128)(2,1)S(1)}, u32[]{:S(2)}, u32[]{:S(2)}) %all-to-all-start.6) | async-done | bytes 2359328 | tf_op jit(solution)/shard_map/all_to_all | solution.py:230
  853.7 1.6 fusion.60
  (84 shorter events, 14.4 us)
Async XLA Ops:
  17.7 18.7 %copy-start.7 = (bf16[4096]{0:T(1024)(128)(2,1)S(1)}, bf16[4096]{0:T(1024)(128)(2,1)}, u32[]{:S(2)}) copy-start(bf16[4096]{0:T(1024)(128)(2,1)} %param.28) | copy-start | bytes 24580
  17.7 18.7 %copy-start.8 = (bf16[4096]{0:T(1024)(128)(2,1)S(1)}, bf16[4096]{0:T(1024)(128)(2,1)}, u32[]{:S(2)}) copy-start(bf16[4096]{0:T(1024)(128)(2,1)} %param.27) | copy-start | bytes 24580
  17.7 421.5 %all-to-all-start.1 = ((bf16[16,8,128,256]{3,2,1,0:T(8,128)(2,1)}), bf16[16,8,128,256]{3,2,1,0:T(8,128)(2,1)}, u32[]{:S(2)}, u32[]{:S(2)}) async-start(bf16[16,8,128,256]{3,2,1,0:T(8,128)(2,1)} %stack.9), calls=%async_computation.1 | async-start | bytes 16777216 | tf_op jit(solution)/shard_map/all_to_all | solution.py:17
  34.9 3.8 copy-start.9
  34.9 4.2 copy-start.6
  34.9 4.3 copy-start.2
  34.9 353.7 %all-gather.2.cloned.1.call-start = ((), (), s32[]{:S(2)}) async-start(), calls=%async_computation.7 | async-start | bytes 4456448 | tf_op jit(solution)/shard_map/all_gather | solution.py:157
  38.6 435.8 %copy-start.3 = (bf16[2,8,8,2048]{3,2,0,1:T(8,128)(2,1)}, bf16[2,8,8,2048]{3,2,0,1:T(8,128)(2,1)S(1)}, u32[]{:S(2)}) copy-start(bf16[2,8,8,2048]{3,2,0,1:T(8,128)(2,1)S(1)} %copy.134) | copy-start | bytes 1572868
  43.3 356.5 %copy-start.5 = (bf16[64,4096,1,1]{1,0,2,3:T(8,128)(2,1)S(1)}, bf16[64,4096,1,1]{1,0,2,3:T(8,128)(2,1)}, u32[]{:S(2)}) copy-start(bf16[64,4096,1,1]{1,0,2,3:T(8,128)(2,1)} %reshape.196) | copy-start | bytes 1572868
  474.1 153.1 %copy-start = (f32[32,4096]{1,0:T(8,128)}, f32[32,4096]{1,0:T(8,128)S(1)}, u32[]{:S(2)}) copy-start(f32[32,4096]{1,0:T(8,128)S(1)} %reduce_sum.105) | copy-start | bytes 1572868
  703.6 9.6 %copy-start.10 = (f32[32,2]{0,1:T(2,128)S(1)}, f32[32,2]{0,1:T(2,128)}, u32[]{:S(2)}) copy-start(f32[32,2]{0,1:T(2,128)} %param.33) | copy-start | bytes 772
  706.7 145.9 %all-to-all-start.6 = ((bf16[16,18,4096]{2,1,0:T(8,128)(2,1)}), bf16[16,18,4096]{2,1,0:T(8,128)(2,1)S(1)}, u32[]{:S(2)}, u32[]{:S(2)}) async-start(bf16[16,18,4096]{2,1,0:T(8,128)(2,1)} %copy.122), calls=%async_computation.6 | async-start | bytes 6291456 | tf_op jit(solution)/shard_map/all_to_all | solution.py:230
  852.5 1.0 copy-start.1
  852.5 1.2 copy-start.4
Sparse Core Ops, SparseCore 0:
  37.4 351.1 all-gather.1
